TPU v7x, 32 devices: a whole 2x2x4 slice. The times are simulated.
32 devices in a mesh: prow: 4 (over y, core), pcol: 8 (over z, x).
Axes of the slice: x: 2, y: 2, z: 4, core: 2. Of those that a mesh axis runs over, the one named last changes fastest.
Arguments:
- matrix: bfloat16 [2, 8, 4, 256, 2, 8, 256], P(None, None, 'prow', None, None, 'pcol'), may hold values from -6 to 6
Outputs:
- image: float32 [2, 8, 4, 256, 2, 8, 256], P(None, None, 'prow', None, None, 'pcol')
All inputs are finite; a program needn't handle non-finite values.
Results may differ from a plain program's by a relative error of at most 0.0003.
Values sent between devices are 32-bit elements; how exact they have to be, the bound alone decides.
A program may use at most 64 MiB of HBM per device.

v0:
```python
import jax
import jax.numpy as jnp
from jax import lax
from jax.sharding import PartitionSpec as P

HIGH = lax.Precision.HIGHEST


def prefix(value, axis, combine, identity):
    length, here = (lax.axis_size(axis), lax.axis_index(axis))
    everything = lax.all_gather(value, axis)
    start = jnp.broadcast_to(jnp.asarray(identity, value.dtype), value.shape)

    def lap(k, before):
        reached = k < here
        new = combine(before, everything[k])
        return jnp.where(reached, new, before)

    return lax.fori_loop(0, length, lap, start)


def add_terms(earlier, later):
    return earlier + later


def shards(matrix):
    batch = matrix.shape[0]
    rows_here = matrix.shape[1]
    tile_len = matrix.shape[3]
    cols_here = matrix.shape[4]
    prow_count = lax.axis_size("prow")
    pcol_count = lax.axis_size("pcol")
    prow_index = lax.axis_index("prow")
    pcol_index = lax.axis_index("pcol")
    local = matrix.astype(jnp.float32).reshape(batch, rows_here, tile_len, cols_here, tile_len)
    first_idx = lax.broadcasted_iota(jnp.int32, (tile_len, tile_len), 0)
    second_idx = lax.broadcasted_iota(jnp.int32, (tile_len, tile_len), 1)
    upper = (first_idx <= second_idx).astype(jnp.float32)
    lower = (second_idx <= first_idx).astype(jnp.float32)
    rowscan = jnp.einsum("nrick,kj->nricj", local, upper, precision=HIGH)
    row_sums = rowscan[:, :, :, :, tile_len - 1]
    gathered = lax.all_gather(row_sums, "pcol", axis=3, tiled=True)
    source = jnp.arange(pcol_count * cols_here, dtype=jnp.int32)
    source_glob = source % cols_here * pcol_count + source // cols_here
    target_glob = jnp.arange(cols_here, dtype=jnp.int32) * pcol_count + pcol_index
    earlier_mask = (source_glob[:, None] < target_glob[None, :]).astype(jnp.float32)
    row_carry = jnp.einsum("nrig,gc->nric", gathered, earlier_mask, precision=HIGH)
    rowscan = rowscan + row_carry[:, :, :, :, None]
    colscan = jnp.einsum("ik,nrkcj->nricj", lower, rowscan, precision=HIGH)
    col_sums = colscan[:, :, tile_len - 1, :, :]
    before = prefix(col_sums, "prow", add_terms, jnp.zeros_like(col_sums))
    whole = lax.psum(col_sums, "prow")
    strict = (jnp.arange(rows_here)[:, None] < jnp.arange(rows_here)[None, :]).astype(jnp.float32)
    col_carry = before + jnp.einsum("nscj,sr->nrcj", whole, strict, precision=HIGH)
    colscan = colscan + col_carry[:, :, None, :, :]
    row_glob = (
        jnp.arange(rows_here, dtype=jnp.int32)[:, None] * prow_count + prow_index
    ) * tile_len + jnp.arange(tile_len, dtype=jnp.int32)[None, :]
    col_glob = (
        jnp.arange(cols_here, dtype=jnp.int32)[:, None] * pcol_count + pcol_index
    ) * tile_len + jnp.arange(tile_len, dtype=jnp.int32)[None, :]
    row_factor = 1.0 / jnp.sqrt(row_glob.astype(jnp.float32) + 1.0)
    col_factor = 1.0 / jnp.sqrt(col_glob.astype(jnp.float32) + 1.0)
    scaled = colscan * (row_factor[None, :, :, None, None] * col_factor[None, None, None, :, :])
    return scaled.reshape(batch, rows_here, 1, tile_len, cols_here, 1, tile_len)


def solution(mesh):
    return jax.shard_map(
        shards,
        mesh=mesh,
        in_specs=(P(None, None, "prow", None, None, "pcol", None),),
        out_specs=P(None, None, "prow", None, None, "pcol", None),
        check_vma=False,
    )
```

profile of v0, /device:TPU:0, one launch (start us, length us, event | category | flops | bytes accessed | tf_op | source)
XLA Modules:
  0.0 76.3 jit_solution(13902189001919219110)
XLA Ops:
  0.0 3.5 %fusion.8 = f32[2,8,256,2,256]{2,4,3,1,0:T(8,128)S(1)} fusion(bf16[2,8,256,2,256]{4,3,2,1,0:T(2,128)(2,1)} %bitcast.44), kind=kOutput, calls=%fused_computation.10 | convolution fusion | flops 1073807360 | bytes 12582912 | tf_op jit(solution)/shard_map/nrick,kj->nricj/dot_general | solution.py:40
  3.5 28.3 %all-gather = f32[2,8,256,16,1]{2,4,3,1,0:T(1,128)S(1)} all-gather(f32[2,8,256,2,1]{2,4,3,1,0:T(1,128)S(1)} %slice.8), channel_id=2, replica_groups=mesh['prow'=4,'pcol'=8] {'pcol'}, dimensions={3}, use_global_device_ids=true | all-gather | bytes 294912 | tf_op jit(solution)/shard_map/all_gather | solution.py:42
  31.9 0.3 fusion.12
  32.2 4.9 %fusion.5 = f32[2,8,256,2,256]{4,2,3,1,0:T(8,128)S(1)} fusion(f32[2,8,256,2,256]{2,4,3,1,0:T(8,128)S(1)} %fusion.8, f32[2,8,256,2]{2,3,1,0:T(2,128)S(1)} %fusion.12), kind=kOutput, calls=%fused_computation.9 | convolution fusion | flops 6444613632 | bytes 16809984 | tf_op jit(solution)/shard_map/ik,nrkcj->nricj/dot_general | solution.py:49
  37.2 0.0 copy-start
  37.2 3.4 %copy-done = f32[2,8,256,2,256]{4,2,3,1,0:T(8,128)} copy-done((f32[2,8,256,2,256]{4,2,3,1,0:T(8,128)}, f32[2,8,256,2,256]{4,2,3,1,0:T(8,128)S(1)}, u32[]{:S(2)}) %copy-start) | copy-done | bytes 8388632
  40.6 5.4 %all-gather.1 = f32[8,8,1,2,256]{4,1,3,2,0:T(8,128)S(1)} all-gather(f32[2,8,1,2,256]{4,1,3,2,0:T(8,128)S(1)} %copy.10), channel_id=3, replica_groups=mesh['prow'=4,'pcol'=8] {'prow'}, dimensions={0}, use_global_device_ids=true | all-gather | bytes 163840 | tf_op jit(solution)/shard_map/all_gather | solution.py:11
  46.0 0.3 while.14
  46.3 11.6 %psum.7 = f32[2,8,2,256]{3,2,1,0:T(2,128)S(1)} all-reduce(f32[2,8,2,256]{3,2,1,0:T(2,128)S(1)} %bitcast.46), channel_id=1, replica_groups=mesh['prow'=4,'pcol'=8] {'prow'}, use_global_device_ids=true, to_apply=%region_2.3 | all-reduce | flops 8192 | bytes 65536 | tf_op jit(solution)/shard_map/psum | solution.py:52
  58.0 0.1 fusion.11
  58.1 0.1 add_rsqrt_fusion
  58.2 0.1 add_rsqrt_fusion.1
  58.3 2.3 %broadcast_multiply_fusion = f32[8,256,2,256]{3,1,2,0:T(8,128)} fusion(f32[2,256]{1,0:T(2,128)S(1)} %add_rsqrt_fusion.1, f32[8,256]{1,0:T(8,128)S(1)} %add_rsqrt_fusion), kind=kLoop, calls=%fused_computation.11 | loop fusion | flops 1048576 | bytes 4204544 | tf_op jit(solution)/shard_map/mul | solution.py:64
  60.6 5.8 %multiply_bitcast_fusion = f32[2,8,1,256,2,1,256]{6,3,4,1,0,5,2:T(8,128)S(1)} fusion(f32[2,8,256,2,256]{4,2,3,1,0:T(8,128)} %copy-done, f32[8,256,2,256]{3,1,2,0:T(8,128)} %broadcast_multiply_fusion, f32[2,8,2,256]{3,2,1,0:T(2,128)S(1)} %copy.14), kind=kLoop, calls=%fused_computation.3 | loop fusion | flops 4194304 | bytes 21004288 | tf_op jit(solution)/shard_map/reshape | solution.py:65
  66.4 9.9 %copy.15 = f32[2,8,1,256,2,1,256]{6,5,4,3,2,1,0:T(1,128)} copy(f32[2,8,1,256,2,1,256]{6,3,4,1,0,5,2:T(8,128)S(1)} %multiply_bitcast_fusion) | data formatting | bytes 16777216 | tf_op jit(solution)/shard_map/reshape | solution.py:65
  (18 shorter events, 0.3 us)
Async XLA Ops:
  37.2 3.4 %copy-start = (f32[2,8,256,2,256]{4,2,3,1,0:T(8,128)}, f32[2,8,256,2,256]{4,2,3,1,0:T(8,128)S(1)}, u32[]{:S(2)}) copy-start(f32[2,8,256,2,256]{4,2,3,1,0:T(8,128)S(1)} %fusion.5) | copy-start | bytes 25165828
where the time goes:
time: 76.5 us; the launch traced here: 76.3 us
  blocking collectives  45.4 us (59%)
  local copies, waits for them, and re-layouts  13.4 us (18%)
  matrix products  8.87 us (12%)
  other arithmetic  8.4 us (11%)
    all_gather x1, blocking collectives, shards(): gathered = lax.all_gather(row_sums, 'pcol', axis=3, tiled=True)  28.3 us
    psum x1, blocking collectives, shards(): whole = lax.psum(col_sums, 'prow')  11.6 us
    reshape x1, local copies, waits for them, and re-layouts, shards(): return scaled.reshape(batch, rows_here, 1, tile_len, cols_here, 1, tile_len)  9.91 us
    reshape x1, other arithmetic, shards(): return scaled.reshape(batch, rows_here, 1, tile_len, cols_here, 1, tile_len)  5.81 us
    all_gather x1, blocking collectives, prefix(): everything = lax.all_gather(value, axis)  5.42 us
    dot_general x1, matrix products, shards(): colscan = jnp.einsum('ik,nrkcj->nricj', lower, rowscan, precision=HIGH)  4.93 us
    dot_general x1, matrix products, shards(): rowscan = jnp.einsum('nrick,kj->nricj', local, upper, precision=HIGH)  3.48 us
    unnamed x3, local copies, waits for them, and re-layouts  3.41 us

commit v1 on v0

v1 whole, which is shorter than its diff:
```python
import functools

import jax
import jax.numpy as jnp
from jax import lax
from jax.experimental import pallas as pl
from jax.experimental.pallas import tpu as pltpu
from jax.sharding import PartitionSpec as P

F32, BF16 = jnp.float32, jnp.bfloat16
HIGH = lax.Precision.HIGHEST
MESH = pl.DeviceIdType.MESH
NN = (((1,), (0,)), ((), ()))
NT = (((1,), (1,)), ((), ()))


def iotas(rows, cols):
    return (lax.broadcasted_iota(jnp.int32, (rows, cols), 0), lax.broadcasted_iota(jnp.int32, (rows, cols), 1))


def dot(a, b, dims=NN, precision=None):
    return lax.dot_general(a, b, dims, precision=precision, preferred_element_type=F32)


def split3(x):
    hi = x.astype(BF16)
    rest = x - hi.astype(F32)
    mid = rest.astype(BF16)
    return hi, mid, (rest - mid.astype(F32)).astype(BF16)


def carries(np_, nq, rows_here, x_hbm, cum_ref, d_ref, xbuf, rs_loc, cs_loc, t_loc, rs_all, cs_all, t_all,
            in_sem, rs_send, rs_recv, cs_send, cs_recv, t_send, t_recv):
    groups, tile, cols, width = x_hbm.shape
    merged = tile * cols
    p, q = lax.axis_index("prow"), lax.axis_index("pcol")
    total = np_ * nq
    me = p * nq + q
    loads = [pltpu.make_async_copy(x_hbm.at[g], xbuf.at[g], in_sem.at[g]) for g in range(groups)]
    for load in loads:
        load.start()

    barrier = pltpu.get_barrier_semaphore()

    def greet(k, _):
        dev = lax.rem(me + k, total)
        pl.semaphore_signal(barrier, inc=1, device_id=(dev // nq, lax.rem(dev, nq)), device_id_type=MESH)
        return 0

    lax.fori_loop(1, total, greet, 0)

    row_g, _ = iotas(groups, width)
    pick_r, pick_l = iotas(groups * cols, merged)
    rs = jnp.zeros((groups, merged), F32)
    cs = jnp.zeros((groups * cols, width), F32)
    for g in range(groups):
        loads[g].wait()
        x = xbuf[g].reshape(merged, width)
        rs = rs + dot((row_g == g).astype(BF16), x, NT)
        cs = cs + dot((pick_r == g * cols + lax.rem(pick_l, cols)).astype(BF16), x)
    rs_loc[...] = rs
    cs_loc[...] = cs
    t_loc[0] = dot(jnp.ones((8, width), F32), jnp.concatenate(
        [cs, jnp.zeros((128 - groups * cols, width), F32)], axis=0), NT, HIGH)[0:1]
    pl.semaphore_wait(barrier, total - 1)

    def rs_copy(k, sender, target):
        return pltpu.make_async_remote_copy(
            src_ref=rs_loc, dst_ref=rs_all.at[sender], send_sem=rs_send.at[k], recv_sem=rs_recv.at[sender],
            device_id=(p, target), device_id_type=MESH)

    def cs_copy(k, sender, target):
        return pltpu.make_async_remote_copy(
            src_ref=cs_loc, dst_ref=cs_all.at[sender], send_sem=cs_send.at[k], recv_sem=cs_recv.at[sender],
            device_id=(target, q), device_id_type=MESH)

    def t_copy(k, sender, target):
        return pltpu.make_async_remote_copy(
            src_ref=t_loc.at[0], dst_ref=t_all.at[sender], send_sem=t_send.at[k], recv_sem=t_recv.at[sender],
            device_id=(target // nq, lax.rem(target, nq)), device_id_type=MESH)

    kinds = ((t_copy, me, total), (cs_copy, p, np_), (rs_copy, q, nq))
    for make, here, count in kinds:
        def send(k, _):
            make(k, here, lax.rem(here + k, count)).start()
            return 0
        lax.fori_loop(1, count, send, 0)

    def drain(make, here, count):
        def wait(k, _):
            make(k, lax.rem(here + k, count), lax.rem(here + k, count)).wait_recv()
            return 0
        lax.fori_loop(1, count, wait, 0)

    drain(*kinds[0])
    t_all[pl.ds(me, 1)] = t_loc[...]

    def t_sum(k, acc):
        a_all, a_lt, b_all, b_lt = acc
        value = t_all[k]
        kp, kq = k // nq, lax.rem(k, nq)
        left = jnp.where(kq < q, value, 0.0)
        up = jnp.where(kp < p, value, 0.0)
        both = jnp.where(kp < p, left, 0.0)
        return a_all + left, a_lt + both, b_all + value, b_lt + up

    zero = jnp.zeros((1, 128), F32)
    a_all, a_lt, b_all, b_lt = lax.fori_loop(0, total, t_sum, (zero,) * 4)
    out, src = iotas(groups * cols, 128)
    out_g, src_g = out // cols, src // cols
    out_c, src_c = lax.rem(out, cols), lax.rem(src, cols)
    same_g = out_g == src_g
    above = (out_g // rows_here == src_g // rows_here) & (src_g < out_g)

    def pair(strict, equal, all_rows, lt_rows):
        wide = jnp.concatenate([jnp.where(above & strict, 1.0, 0.0), jnp.where(same_g & strict, 1.0, 0.0)], axis=1)
        return jnp.sum(wide * jnp.concatenate([all_rows, lt_rows], axis=1), axis=1, keepdims=True)

    corner = pair(src_c == out_c, None, a_all, a_lt) + pair(src_c < out_c, None, b_all, b_lt)

    drain(*kinds[1])
    c_all, c_lt = cs, jnp.zeros_like(cs)
    for k in range(np_):
        value = jnp.where(k == p, 0.0, cs_all[k])
        c_all = c_all + value
        c_lt = c_lt + jnp.where(k < p, value, 0.0)
    o, s = iotas(groups * cols, groups * cols)
    strict = ((o // (rows_here * cols) == s // (rows_here * cols)) & (lax.rem(o, cols) == lax.rem(s, cols))
              & (s // cols < o // cols)).astype(F32)
    pre = dot(strict, c_all, NN, HIGH) + c_lt
    u0, u1 = iotas(width, width)
    d_ref[...] = dot(pre, (u0 <= u1).astype(F32), NN, HIGH) + corner

    i0, i1 = iotas(merged, merged)
    reach = i1 // cols <= i0 // cols
    c0, c1 = lax.rem(i0, cols), lax.rem(i1, cols)
    low = (reach & (c0 == c1)).astype(BF16)
    low_all = (reach & (c1 < c0)).astype(BF16)
    drain(*kinds[2])
    r_all, r_lt = rs, jnp.zeros_like(rs)
    for k in range(nq):
        value = jnp.where(k == q, 0.0, rs_all[k])
        r_all = r_all + value
        r_lt = r_lt + jnp.where(k < q, value, 0.0)
    cum = jnp.zeros((merged, groups), F32)
    for part_lt, part_all in zip(split3(r_lt), split3(r_all)):
        cum = cum + dot(low, part_lt, NT) + dot(low_all, part_all, NT)
    parts = split3(cum)
    cum_ref[...] = jnp.concatenate(
        [*(part.astype(F32) for part in parts), jnp.zeros((merged, 128 - 3 * groups), F32)], axis=1).astype(BF16)

    for make, here, count in kinds:
        def sent(k, _):
            make(k, here, lax.rem(here + k, count)).wait_send()
            return 0
        lax.fori_loop(1, count, sent, 0)


def finish(np_, nq, rows_here, groups, x_ref, cum_ref, d_ref, o_ref, low_ref, up_ref, cf_ref):
    tile, cols, width = x_ref.shape
    merged = tile * cols
    g = pl.program_id(0)
    p, q = lax.axis_index("prow"), lax.axis_index("pcol")

    @pl.when(g == 0)
    def _():
        i0, i1 = iotas(merged, merged)
        low_ref[...] = ((i1 <= i0) & (lax.rem(i0 - i1 + merged, cols) == 0)).astype(BF16)
        u0, u1 = iotas(width, width)
        up_ref[...] = (u0 <= u1).astype(BF16)
        c0, c1 = iotas(8, width)
        cf_ref[...] = 1.0 / jnp.sqrt((((lax.rem(c0, cols) * nq + q) * width + c1) + 1).astype(F32))

    x = x_ref[...].reshape(merged, width)
    y = dot(low_ref[...], x)
    hi = y.astype(BF16)
    lo = (y - hi.astype(F32)).astype(BF16)
    l0, _ = iotas(128, width)
    pick = ((lax.rem(l0, groups) == g) & (l0 < 3 * groups)).astype(BF16)
    s = dot(hi, up_ref[...]) + dot(lo, up_ref[...]) + dot(cum_ref[...], pick)
    d = d_ref[...].reshape(cols, width)
    dd = jnp.concatenate([d] * (8 // cols), axis=0)
    a0, _ = iotas(merged, 128)
    rf = 1.0 / jnp.sqrt((((lax.rem(g, rows_here) * np_ + p) * tile + a0 // cols) + 1).astype(F32))
    for t in range(width // 128):
        cut = slice(t * 128, (t + 1) * 128)
        part = s[:, cut].reshape(merged // 8, 8, 128) + dd[None, :, cut]
        part = part * (rf.reshape(merged // 8, 8, 128) * cf_ref[:, cut][None])
        o_ref[pl.ds(t, merged, stride=width // 128), :] = part.reshape(merged, 128)


def solution(mesh):
    np_, nq = mesh.shape["prow"], mesh.shape["pcol"]

    def shards(matrix):
        batch, rows_here, _, tile, cols, _, width = matrix.shape
        groups, merged, lanes = batch * rows_here, tile * cols, width // 128
        x = matrix.reshape(groups, tile, cols, width)
        dma = pltpu.SemaphoreType.DMA
        vmem = pl.BlockSpec(memory_space=pltpu.VMEM)
        total = np_ * nq
        cum, d = pl.pallas_call(
            functools.partial(carries, np_, nq, rows_here),
            out_shape=(jax.ShapeDtypeStruct((merged, 128), BF16), jax.ShapeDtypeStruct((groups * cols, width), F32)),
            in_specs=[pl.BlockSpec(memory_space=pl.ANY)],
            out_specs=(vmem, vmem),
            scratch_shapes=[
                pltpu.VMEM((groups, tile, cols, width), BF16),
                pltpu.VMEM((groups, merged), F32),
                pltpu.VMEM((groups * cols, width), F32),
                pltpu.VMEM((1, 1, 128), F32),
                pltpu.VMEM((nq, groups, merged), F32),
                pltpu.VMEM((np_, groups * cols, width), F32),
                pltpu.VMEM((total, 1, 128), F32),
                dma((groups,)), dma((nq,)), dma((nq,)), dma((np_,)), dma((np_,)), dma((total,)), dma((total,)),
            ],
            compiler_params=pltpu.CompilerParams(
                collective_id=0, has_side_effects=True, vmem_limit_bytes=40 * 2**20),
            name="carries",
        )(x)
        out = pl.pallas_call(
            functools.partial(finish, np_, nq, rows_here, groups),
            grid=(groups,),
            out_shape=jax.ShapeDtypeStruct((groups, merged * lanes, 128), F32),
            in_specs=[
                pl.BlockSpec((None, tile, cols, width), lambda g: (g, 0, 0, 0)),
                pl.BlockSpec((merged, 128), lambda g: (0, 0)),
                pl.BlockSpec((None, cols, width), lambda g: (g, 0, 0)),
            ],
            out_specs=pl.BlockSpec((None, merged * lanes, 128), lambda g: (g, 0, 0)),
            scratch_shapes=[pltpu.VMEM((merged, merged), BF16), pltpu.VMEM((width, width), BF16),
                            pltpu.VMEM((8, width), F32)],
            name="finish",
        )(x, cum, d.reshape(groups, cols, width))
        return out.reshape(matrix.shape)

    spec = P(None, None, "prow", None, None, "pcol", None)
    return jax.shard_map(shards, mesh=mesh, in_specs=(spec,), out_specs=spec, check_vma=False)
```

time: 76.5 us -> 38.5 us (0.50)
  blocking collectives: 45.4 us -> 0 us
  Pallas kernels: 0 us -> 34.5 us
  local copies, waits for them, and re-layouts: 13.4 us -> 3.46 us
  matrix products: 8.87 us -> 0 us
  other arithmetic: 8.4 us -> 0 us
    pallas_call x0 -> x2, Pallas kernels: none -> 34.5 us  [the longest x1 17.7 us: shards(): pl.pallas_call(functools.partial(finish, np_, nq, rows_here, groups), gri...]
    all_gather x2 -> x0, blocking collectives: 33.8 us -> none  [the longest x1 28.3 us: shards(): gathered = lax.all_gather(row_sums, 'pcol', axis=3, tiled=True)]
    psum x1 -> x0, blocking collectives: 11.6 us -> none  [shards(): whole = lax.psum(col_sums, 'prow')]
    reshape x1, local copies, waits for them, and re-layouts: 9.91 us -> 0.64 us  [shards(): d.reshape(groups, cols, width)]
    dot_general x4 -> x0, matrix products: 8.87 us -> none  [the longest x1 4.93 us: shards(): colscan = jnp.einsum('ik,nrkcj->nricj', lower, rowscan, precision=HIGH)]
    reshape x1 -> x0, other arithmetic: 5.81 us -> none  [shards(): return scaled.reshape(batch, rows_here, 1, tile_len, cols_here, 1, tile_len)]
    mul x3 -> x0, other arithmetic: 2.28 us -> none  [the longest x1 2.27 us: shards(): row_factor[None, :, :, None, None] * col_factor[None, None, None, :, :]]
    unnamed x3 -> x4, local copies, waits for them, and re-layouts: 3.41 us -> 2.83 us
where the time goes in v1:
time: 38.5 us; the launch traced here: 37.9 us
  Pallas kernels  34.5 us (90%)
  local copies, waits for them, and re-layouts  3.46 us (9%)
    pallas_call x1, Pallas kernels, shards(): pl.pallas_call(functools.partial(finish, np_, nq, rows_here, groups), gri...  17.7 us
    pallas_call x1, Pallas kernels, shards(): pl.pallas_call(functools.partial(carries, np_, nq, rows_here), out_shape=...  16.7 us
    unnamed x4, local copies, waits for them, and re-layouts  2.83 us

profile of v1, /device:TPU:0, one launch (start us, length us, event | category | flops | bytes accessed | tf_op | source)
XLA Modules:
  0.0 37.9 jit_solution(17615847731895401710)
XLA Ops:
  0.0 0.0 copy-start
  0.0 2.2 %copy-done = bf16[2,8,1,256,2,1,256]{6,4,5,3,2,1,0:T(2,128)(2,1)S(1)} copy-done((bf16[2,8,1,256,2,1,256]{6,4,5,3,2,1,0:T(2,128)(2,1)S(1)}, bf16[2,8,1,256,2,1,256]{6,4,5,3,2,1,0:T(2,128)(2,1)}, u32[]{:S(2)}) %copy-start) | copy-done | bytes 4194328
  2.2 16.7 %carries.1 = (bf16[512,128]{1,0:T(8,128)(2,1)S(1)}, f32[32,256]{1,0:T(8,128)S(1)}) custom-call(bf16[16,256,2,256]{3,2,1,0:T(2,128)(2,1)S(1)} %bitcast.3), custom_call_target="tpu_custom_call" | custom-call | tf_op jit(solution)/shard_map/carries/pallas_call | solution.py:202
  18.9 0.0 copy-start.1
  18.9 0.6 %copy-done.1 = bf16[512,128]{1,0:T(8,128)(2,1)} copy-done((bf16[512,128]{1,0:T(8,128)(2,1)}, bf16[512,128]{1,0:T(8,128)(2,1)S(1)}, u32[]{:S(2)}) %copy-start.1) | copy-done | bytes 131096
  19.6 0.6 %reshape.10.d_ref = f32[16,2,256]{2,1,0:T(2,128)} reshape(f32[32,256]{1,0:T(8,128)S(1)} %get-tuple-element.8) | data formatting | bytes 65536 | tf_op jit(solution)/shard_map/reshape | solution.py:234
  20.2 17.7 %finish.1 = f32[16,1024,128]{2,1,0:T(8,128)} custom-call(bf16[16,256,2,256]{3,2,1,0:T(2,128)(2,1)} %bitcast.2, bf16[512,128]{1,0:T(8,128)(2,1)} %copy-done.1, f32[16,2,256]{2,1,0:T(2,128)} %reshape.10.d_ref), custom_call_target="tpu_custom_call" | custom-call | tf_op jit(solution)/shard_map/finish/pallas_call | solution.py:221
Async XLA Ops:
  0.0 2.2 %copy-start = (bf16[2,8,1,256,2,1,256]{6,4,5,3,2,1,0:T(2,128)(2,1)S(1)}, bf16[2,8,1,256,2,1,256]{6,4,5,3,2,1,0:T(2,128)(2,1)}, u32[]{:S(2)}) copy-start(bf16[2,8,1,256,2,1,256]{6,4,5,3,2,1,0:T(2,128)(2,1)} %param.1) | copy-start | bytes 12582916
  18.9 0.6 %copy-start.1 = (bf16[512,128]{1,0:T(8,128)(2,1)}, bf16[512,128]{1,0:T(8,128)(2,1)S(1)}, u32[]{:S(2)}) copy-start(bf16[512,128]{1,0:T(8,128)(2,1)S(1)} %get-tuple-element.7.cum_ref) | copy-start | bytes 393220

commit v2 on v1

--- a/solution.py
+++ b/solution.py
@@ -80,7 +80,7 @@
             device_id=(target // nq, lax.rem(target, nq)), device_id_type=MESH)
 
     kinds = ((t_copy, me, total), (cs_copy, p, np_), (rs_copy, q, nq))
-    for make, here, count in kinds:
+    for make, here, count in kinds[::-1]:
         def send(k, _):
             make(k, here, lax.rem(here + k, count)).start()
             return 0
@@ -169,7 +169,7 @@
         u0, u1 = iotas(width, width)
         up_ref[...] = (u0 <= u1).astype(BF16)
         c0, c1 = iotas(8, width)
-        cf_ref[...] = 1.0 / jnp.sqrt((((lax.rem(c0, cols) * nq + q) * width + c1) + 1).astype(F32))
+        cf_ref[...] = lax.rsqrt((((lax.rem(c0, cols) * nq + q) * width + c1) + 1).astype(F32))
 
     x = x_ref[...].reshape(merged, width)
     y = dot(low_ref[...], x)
@@ -181,7 +181,7 @@
     d = d_ref[...].reshape(cols, width)
     dd = jnp.concatenate([d] * (8 // cols), axis=0)
     a0, _ = iotas(merged, 128)
-    rf = 1.0 / jnp.sqrt((((lax.rem(g, rows_here) * np_ + p) * tile + a0 // cols) + 1).astype(F32))
+    rf = lax.rsqrt((((lax.rem(g, rows_here) * np_ + p) * tile + a0 // cols) + 1).astype(F32))
     for t in range(width // 128):
         cut = slice(t * 128, (t + 1) * 128)
         part = s[:, cut].reshape(merged // 8, 8, 128) + dd[None, :, cut]

time: 38.5 us -> 41.6 us (1.081)
  Pallas kernels: 34.5 us -> 37.6 us
    pallas_call x1, Pallas kernels: 16.7 us -> 19.9 us  [shards(): pl.pallas_call(functools.partial(carries, np_, nq, rows_here), out_shape=...]
where the time goes in v2:
time: 41.6 us; the launch traced here: 41 us
  Pallas kernels  37.6 us (90%)
  local copies, waits for them, and re-layouts  3.46 us (8%)
    pallas_call x1, Pallas kernels, shards(): pl.pallas_call(functools.partial(carries, np_, nq, rows_here), out_shape=...  19.9 us
    pallas_call x1, Pallas kernels, shards(): pl.pallas_call(functools.partial(finish, np_, nq, rows_here, groups), gri...  17.7 us
    unnamed x4, local copies, waits for them, and re-layouts  2.83 us

profile of v2, /device:TPU:0, one launch (start us, length us, event | category | flops | bytes accessed | tf_op | source)
XLA Modules:
  0.0 41.0 jit_solution(2529955182127374740)
XLA Ops:
  0.0 0.0 copy-start
  0.0 2.2 %copy-done = bf16[2,8,1,256,2,1,256]{6,4,5,3,2,1,0:T(2,128)(2,1)S(1)} copy-done((bf16[2,8,1,256,2,1,256]{6,4,5,3,2,1,0:T(2,128)(2,1)S(1)}, bf16[2,8,1,256,2,1,256]{6,4,5,3,2,1,0:T(2,128)(2,1)}, u32[]{:S(2)}) %copy-start) | copy-done | bytes 4194328
  2.2 19.9 %carries.1 = (bf16[512,128]{1,0:T(8,128)(2,1)S(1)}, f32[32,256]{1,0:T(8,128)S(1)}) custom-call(bf16[16,256,2,256]{3,2,1,0:T(2,128)(2,1)S(1)} %bitcast.3), custom_call_target="tpu_custom_call" | custom-call | tf_op jit(solution)/shard_map/carries/pallas_call | solution.py:202
  22.1 0.0 copy-start.1
  22.1 0.6 %copy-done.1 = bf16[512,128]{1,0:T(8,128)(2,1)} copy-done((bf16[512,128]{1,0:T(8,128)(2,1)}, bf16[512,128]{1,0:T(8,128)(2,1)S(1)}, u32[]{:S(2)}) %copy-start.1) | copy-done | bytes 131096
  22.7 0.6 %reshape.10.d_ref = f32[16,2,256]{2,1,0:T(2,128)} reshape(f32[32,256]{1,0:T(8,128)S(1)} %get-tuple-element.8) | data formatting | bytes 65536 | tf_op jit(solution)/shard_map/reshape | solution.py:234
  23.3 17.7 %finish.1 = f32[16,1024,128]{2,1,0:T(8,128)} custom-call(bf16[16,256,2,256]{3,2,1,0:T(2,128)(2,1)} %bitcast.2, bf16[512,128]{1,0:T(8,128)(2,1)} %copy-done.1, f32[16,2,256]{2,1,0:T(2,128)} %reshape.10.d_ref), custom_call_target="tpu_custom_call" | custom-call | tf_op jit(solution)/shard_map/finish/pallas_call | solution.py:221
Async XLA Ops:
  0.0 2.2 %copy-start = (bf16[2,8,1,256,2,1,256]{6,4,5,3,2,1,0:T(2,128)(2,1)S(1)}, bf16[2,8,1,256,2,1,256]{6,4,5,3,2,1,0:T(2,128)(2,1)}, u32[]{:S(2)}) copy-start(bf16[2,8,1,256,2,1,256]{6,4,5,3,2,1,0:T(2,128)(2,1)} %param.1) | copy-start | bytes 12582916
  22.1 0.6 %copy-start.1 = (bf16[512,128]{1,0:T(8,128)(2,1)}, bf16[512,128]{1,0:T(8,128)(2,1)S(1)}, u32[]{:S(2)}) copy-start(bf16[512,128]{1,0:T(8,128)(2,1)S(1)} %get-tuple-element.7.cum_ref) | copy-start | bytes 393220

commit v3 on v2

--- a/solution.py
+++ b/solution.py
@@ -29,7 +29,7 @@
     return hi, mid, (rest - mid.astype(F32)).astype(BF16)
 
 
-def carries(np_, nq, rows_here, x_hbm, cum_ref, d_ref, xbuf, rs_loc, cs_loc, t_loc, rs_all, cs_all, t_all,
+def carries(np_, nq, rows_here, x_hbm, cum_ref, d_ref, flat_ref, xbuf, rs_loc, cs_loc, t_loc, rs_all, cs_all, t_all,
             in_sem, rs_send, rs_recv, cs_send, cs_recv, t_send, t_recv):
     groups, tile, cols, width = x_hbm.shape
     merged = tile * cols
@@ -56,6 +56,7 @@
     for g in range(groups):
         loads[g].wait()
         x = xbuf[g].reshape(merged, width)
+        flat_ref[g] = x
         rs = rs + dot((row_g == g).astype(BF16), x, NT)
         cs = cs + dot((pick_r == g * cols + lax.rem(pick_l, cols)).astype(BF16), x)
     rs_loc[...] = rs
@@ -80,7 +81,7 @@
             device_id=(target // nq, lax.rem(target, nq)), device_id_type=MESH)
 
     kinds = ((t_copy, me, total), (cs_copy, p, np_), (rs_copy, q, nq))
-    for make, here, count in kinds[::-1]:
+    for make, here, count in kinds:
         def send(k, _):
             make(k, here, lax.rem(here + k, count)).start()
             return 0
@@ -129,7 +130,7 @@
               & (s // cols < o // cols)).astype(F32)
     pre = dot(strict, c_all, NN, HIGH) + c_lt
     u0, u1 = iotas(width, width)
-    d_ref[...] = dot(pre, (u0 <= u1).astype(F32), NN, HIGH) + corner
+    d_ref[...] = (dot(pre, (u0 <= u1).astype(F32), NN, HIGH) + corner).reshape(groups, cols, width)
 
     i0, i1 = iotas(merged, merged)
     reach = i1 // cols <= i0 // cols
@@ -157,8 +158,9 @@
 
 
 def finish(np_, nq, rows_here, groups, x_ref, cum_ref, d_ref, o_ref, low_ref, up_ref, cf_ref):
-    tile, cols, width = x_ref.shape
-    merged = tile * cols
+    merged, width = x_ref.shape
+    cols = d_ref.shape[0]
+    tile = merged // cols
     g = pl.program_id(0)
     p, q = lax.axis_index("prow"), lax.axis_index("pcol")
 
@@ -171,7 +173,7 @@
         c0, c1 = iotas(8, width)
         cf_ref[...] = lax.rsqrt((((lax.rem(c0, cols) * nq + q) * width + c1) + 1).astype(F32))
 
-    x = x_ref[...].reshape(merged, width)
+    x = x_ref[...]
     y = dot(low_ref[...], x)
     hi = y.astype(BF16)
     lo = (y - hi.astype(F32)).astype(BF16)
@@ -199,11 +201,12 @@
         dma = pltpu.SemaphoreType.DMA
         vmem = pl.BlockSpec(memory_space=pltpu.VMEM)
         total = np_ * nq
-        cum, d = pl.pallas_call(
+        cum, d, flat = pl.pallas_call(
             functools.partial(carries, np_, nq, rows_here),
-            out_shape=(jax.ShapeDtypeStruct((merged, 128), BF16), jax.ShapeDtypeStruct((groups * cols, width), F32)),
+            out_shape=(jax.ShapeDtypeStruct((merged, 128), BF16), jax.ShapeDtypeStruct((groups, cols, width), F32),
+                       jax.ShapeDtypeStruct((groups, merged, width), BF16)),
             in_specs=[pl.BlockSpec(memory_space=pl.ANY)],
-            out_specs=(vmem, vmem),
+            out_specs=(vmem, vmem, vmem),
             scratch_shapes=[
                 pltpu.VMEM((groups, tile, cols, width), BF16),
                 pltpu.VMEM((groups, merged), F32),
@@ -223,7 +226,7 @@
             grid=(groups,),
             out_shape=jax.ShapeDtypeStruct((groups, merged * lanes, 128), F32),
             in_specs=[
-                pl.BlockSpec((None, tile, cols, width), lambda g: (g, 0, 0, 0)),
+                pl.BlockSpec((None, merged, width), lambda g: (g, 0, 0)),
                 pl.BlockSpec((merged, 128), lambda g: (0, 0)),
                 pl.BlockSpec((None, cols, width), lambda g: (g, 0, 0)),
             ],
@@ -231,7 +234,7 @@
             scratch_shapes=[pltpu.VMEM((merged, merged), BF16), pltpu.VMEM((width, width), BF16),
                             pltpu.VMEM((8, width), F32)],
             name="finish",
-        )(x, cum, d.reshape(groups, cols, width))
+        )(flat, cum, d)
         return out.reshape(matrix.shape)
 
     spec = P(None, None, "prow", None, None, "pcol", None)

time: 41.6 us -> 40.3 us (0.969)
  Pallas kernels: 37.6 us -> 34.4 us
  local copies, waits for them, and re-layouts: 3.46 us -> 5.38 us
    pallas_call x1, Pallas kernels: 19.9 us -> 16.8 us  [shards(): pl.pallas_call(functools.partial(carries, np_, nq, rows_here), out_shape=...]
    unnamed x4 -> x8, local copies, waits for them, and re-layouts: 2.83 us -> 5.38 us
    reshape x1 -> x0, local copies, waits for them, and re-layouts: 0.64 us -> none  [shards(): d.reshape(groups, cols, width)]
where the time goes in v3:
time: 40.3 us; the launch traced here: 39.8 us
  Pallas kernels  34.4 us (85%)
  local copies, waits for them, and re-layouts  5.38 us (13%)
    pallas_call x1, Pallas kernels, shards(): pl.pallas_call(functools.partial(finish, np_, nq, rows_here, groups), gri...  17.6 us
    pallas_call x1, Pallas kernels, shards(): pl.pallas_call(functools.partial(carries, np_, nq, rows_here), out_shape=...  16.8 us
    unnamed x8, local copies, waits for them, and re-layouts  5.38 us

profile of v3, /device:TPU:0, one launch (start us, length us, event | category | flops | bytes accessed | tf_op | source)
XLA Modules:
  0.0 39.8 jit_solution(16716794799735904508)
XLA Ops:
  0.0 0.0 copy-start.1
  0.0 2.2 %copy-done.1 = bf16[2,8,1,256,2,1,256]{6,4,5,3,2,1,0:T(2,128)(2,1)S(1)} copy-done((bf16[2,8,1,256,2,1,256]{6,4,5,3,2,1,0:T(2,128)(2,1)S(1)}, bf16[2,8,1,256,2,1,256]{6,4,5,3,2,1,0:T(2,128)(2,1)}, u32[]{:S(2)}) %copy-start.1) | copy-done | bytes 4194328
  2.2 16.8 %carries.1 = (bf16[512,128]{1,0:T(8,128)(2,1)S(1)}, f32[16,2,256]{2,1,0:T(2,128)S(1)}, bf16[16,512,256]{2,1,0:T(8,128)(2,1)S(1)}) custom-call(bf16[16,256,2,256]{3,2,1,0:T(2,128)(2,1)S(1)} %bitcast.2), custom_call_target="tpu_custom_call" | custom-call | tf_op jit(solution)/shard_map/carries/pallas_call | solution.py:204
  19.0 0.0 copy-start
  19.0 1.9 %copy-done = bf16[16,512,256]{2,1,0:T(8,128)(2,1)} copy-done((bf16[16,512,256]{2,1,0:T(8,128)(2,1)}, bf16[16,512,256]{2,1,0:T(8,128)(2,1)S(1)}, u32[]{:S(2)}) %copy-start) | copy-done | bytes 4194328
  20.9 0.0 copy-start.2
  20.9 0.6 %copy-done.2 = bf16[512,128]{1,0:T(8,128)(2,1)} copy-done((bf16[512,128]{1,0:T(8,128)(2,1)}, bf16[512,128]{1,0:T(8,128)(2,1)S(1)}, u32[]{:S(2)}) %copy-start.2) | copy-done | bytes 131096
  21.6 0.0 copy-start.3
  21.6 0.6 %copy-done.3 = f32[16,2,256]{2,1,0:T(2,128)} copy-done((f32[16,2,256]{2,1,0:T(2,128)}, f32[16,2,256]{2,1,0:T(2,128)S(1)}, u32[]{:S(2)}) %copy-start.3) | copy-done | bytes 32792
  22.2 17.6 %finish.1 = f32[16,1024,128]{2,1,0:T(8,128)} custom-call(bf16[16,512,256]{2,1,0:T(8,128)(2,1)} %copy-done, bf16[512,128]{1,0:T(8,128)(2,1)} %copy-done.2, f32[16,2,256]{2,1,0:T(2,128)} %copy-done.3), custom_call_target="tpu_custom_call" | custom-call | tf_op jit(solution)/shard_map/finish/pallas_call | solution.py:224
Async XLA Ops:
  0.0 2.2 %copy-start.1 = (bf16[2,8,1,256,2,1,256]{6,4,5,3,2,1,0:T(2,128)(2,1)S(1)}, bf16[2,8,1,256,2,1,256]{6,4,5,3,2,1,0:T(2,128)(2,1)}, u32[]{:S(2)}) copy-start(bf16[2,8,1,256,2,1,256]{6,4,5,3,2,1,0:T(2,128)(2,1)} %param.1) | copy-start | bytes 12582916
  19.0 1.9 %copy-start = (bf16[16,512,256]{2,1,0:T(8,128)(2,1)}, bf16[16,512,256]{2,1,0:T(8,128)(2,1)S(1)}, u32[]{:S(2)}) copy-start(bf16[16,512,256]{2,1,0:T(8,128)(2,1)S(1)} %get-tuple-element.8.x_ref) | copy-start | bytes 12582916
  20.9 0.6 %copy-start.2 = (bf16[512,128]{1,0:T(8,128)(2,1)}, bf16[512,128]{1,0:T(8,128)(2,1)S(1)}, u32[]{:S(2)}) copy-start(bf16[512,128]{1,0:T(8,128)(2,1)S(1)} %get-tuple-element.9.cum_ref) | copy-start | bytes 393220
  21.6 0.6 %copy-start.3 = (f32[16,2,256]{2,1,0:T(2,128)}, f32[16,2,256]{2,1,0:T(2,128)S(1)}, u32[]{:S(2)}) copy-start(f32[16,2,256]{2,1,0:T(2,128)S(1)} %get-tuple-element.10.d_ref) | copy-start | bytes 98308
